TPU v7x, 32 devices: a whole 2x2x4 slice. The times are simulated.
32 devices in a mesh: traj: 4 (over y, x), grid: 8 (over z, core).
Axes of the slice: x: 2, y: 2, z: 4, core: 2. Of those that a mesh axis runs over, the one named last changes fastest.
Arguments:
- psi_modes: float32 [4, 2, 256, 256, 256], P('traj', None, None, 'grid'), may hold values from -6 to 6
- noise: float32 [4, 2, 256, 256, 256], P('traj', None, 'grid'), may hold values from -6 to 6
- mask: int32 [256, 256, 256], P(None, 'grid'), may hold values from 0 to 1, as said below
Outputs:
- psi_next: float32 [4, 2, 256, 256, 256], P('traj', None, None, 'grid')
- momentum_hist: float32 [128], replicated
Inputs may be any that keep to these rules, and one draw needn't show every extreme that they name: mask is 0 at every mode whose signed third index has magnitude 256/4 or more, and 1 at some mode whose signed third index has magnitude 256/4 - 1.
All inputs are finite; a program needn't handle non-finite values.
Results may differ from a plain program's by a relative error of at most 0.00023.
Values sent between devices are 32-bit elements; how exact they have to be, the bound alone decides.
A program may use at most 192 MiB of HBM per device.

v0:
```python
import jax
import jax.numpy as jnp
from jax import lax
from jax.sharding import PartitionSpec as P

SHELLS = 128
time_step = 1.0
damping = 0.05
coupling = 10.0
chem_potential = 1.0
noise_amp = 0.1
trap_strength = 8.0
max_chunks = 4


def signed_of(index, count):
    return jnp.where(index < count // 2, index, index - count)


def dft_table(out_index, in_index, count, sign):
    phase = (out_index[:, None] * in_index[None, :] % count).astype(jnp.float32) * (
        2.0 * jnp.pi / count
    )
    scale = 1.0 / jnp.sqrt(jnp.float32(count))
    return (jnp.cos(phase) * scale, sign * jnp.sin(phase) * scale)


def axis_factor(modes, count):
    wave = modes.astype(jnp.float32) * (2.0 * jnp.pi / count)
    theta = 0.25 * time_step * wave * wave
    size = jnp.exp(-damping * theta)
    return (size * jnp.cos(theta), -size * jnp.sin(theta))


def scaled(table, factor, dim):
    real, imag = factor
    if dim == 0:
        real, imag = (real[:, None], imag[:, None])
    else:
        real, imag = (real[None, :], imag[None, :])
    return (table[0] * real - table[1] * imag, table[0] * imag + table[1] * real)


def block_table(table):
    real, imag = table
    top = jnp.stack([real, -imag], axis=1)
    bottom = jnp.stack([imag, real], axis=1)
    return jnp.stack([top, bottom], axis=0)


def contract(pattern, table, values):
    return jnp.einsum(pattern, table, values, precision=lax.Precision.HIGH)


def cos_sin(angle):
    turns = jnp.round(angle * (2.0 / jnp.pi))
    rest = angle - turns * 1.5703125
    rest = rest - turns * 0.0004837512969970703
    rest = rest - turns * 7.549789954891882e-08
    sq = rest * rest
    sine = rest + rest * sq * (-0.16666654611 + sq * (0.0083321608736 + sq * -0.00019515295891))
    cosine = 1.0 + sq * (
        -0.5
        + sq * (0.04166664568298827 + sq * (-0.001388731625493765 + sq * 2.443315711809948e-05))
    )
    quadrant = turns.astype(jnp.int32)
    odd = quadrant & 1 != 0
    cos_out = jnp.where(odd, sine, cosine)
    sin_out = jnp.where(odd, cosine, sine)
    cos_out = jnp.where(quadrant + 1 & 2 != 0, -cos_out, cos_out)
    sin_out = jnp.where(quadrant & 2 != 0, -sin_out, sin_out)
    return (cos_out, sin_out)


def shell_sums(occupation, modes_x, modes_y, modes_z, limit):
    base = (modes_x[:, None] ** 2 + modes_y[None, :] ** 2) * SHELLS
    row_shell = jnp.minimum(base // limit, SHELLS - 1).reshape(-1)
    row_rest = (base % limit).reshape(-1)
    col = modes_z**2 * SHELLS
    col_shell = col // limit
    col_rest = col % limit
    flat = occupation.reshape(row_rest.shape[0], -1)
    carry = row_rest[:, None] + col_rest[None, :] >= limit
    zero = jnp.float32(0.0)
    both = jnp.concatenate([jnp.where(carry, zero, flat), jnp.where(carry, flat, zero)], axis=-1)
    shell_ids = jnp.arange(SHELLS, dtype=jnp.int32)
    hits = (row_shell[None, :] == shell_ids[:, None]).astype(jnp.float32)
    sums = jnp.einsum("sr,rc->sc", hits, both, precision=lax.Precision.HIGHEST)
    offset = jnp.concatenate([col_shell, col_shell + 1])
    shell = jnp.minimum(shell_ids[:, None] + offset[None, :], SHELLS - 1)
    picked = jnp.where(shell[None] == shell_ids[:, None, None], sums[None], zero)
    return jnp.sum(picked, axis=(1, 2))


def shards(psi_modes, noise, mask):
    grid_rank = lax.axis_index("grid")
    ranks = lax.axis_size("grid")
    extent_x = mask.shape[0]
    extent_y = noise.shape[3]
    extent_z = mask.shape[2]
    rows_local = mask.shape[1]
    planes_local = noise.shape[2]
    quarter = extent_z // 4
    chunks = max_chunks
    while planes_local % chunks:
        chunks -= 1
    depth = planes_local // chunks

    def select_cols(values):
        return jnp.concatenate([values[..., :quarter], values[..., extent_z - quarter :]], axis=-1)

    index_x, index_y, all_cols = lax.optimization_barrier(
        tuple((jnp.arange(extent, dtype=jnp.int32) for extent in (extent_x, extent_y, extent_z)))
    )
    column_ids = select_cols(all_cols)
    modes_x = signed_of(index_x, extent_x)
    modes_y_all = signed_of(index_y, extent_y)
    modes_y = signed_of(grid_rank * rows_local + jnp.arange(rows_local, dtype=jnp.int32), extent_y)
    modes_z = signed_of(column_ids, extent_z)
    fac_x = axis_factor(modes_x, extent_x)
    fac_y = axis_factor(modes_y_all, extent_y)
    fac_z = axis_factor(modes_z, extent_z)
    inverse_x = block_table(scaled(dft_table(index_x, index_x, extent_x, 1.0), fac_x, 1))
    inverse_y = block_table(scaled(dft_table(index_y, index_y, extent_y, 1.0), fac_y, 1))
    inverse_z = block_table(scaled(dft_table(all_cols, column_ids, extent_z, 1.0), fac_z, 1))
    forward_x = block_table(scaled(dft_table(index_x, index_x, extent_x, -1.0), fac_x, 0))
    forward_y = block_table(scaled(dft_table(index_y, index_y, extent_y, -1.0), fac_y, 0))
    forward_z = block_table(scaled(dft_table(column_ids, all_cols, extent_z, -1.0), fac_z, 0))
    inverse_x = inverse_x.reshape(2, ranks, chunks, depth, 2, extent_x)
    inverse_y = inverse_y.reshape(2, extent_y, 2, ranks, rows_local)
    forward_y = forward_y.reshape(2, ranks, rows_local, 2, extent_y)
    forward_x = forward_x.reshape(2, extent_x, 2, ranks, chunks, depth)
    kept = select_cols(mask).astype(jnp.float32)
    start = select_cols(psi_modes) * kept
    pos_x = (grid_rank * planes_local + jnp.arange(planes_local, dtype=jnp.int32)).astype(
        jnp.float32
    )
    pos_x = (pos_x + 0.5) / extent_x - 0.5
    pos_y = (index_y.astype(jnp.float32) + 0.5) / extent_y - 0.5
    pos_z = (all_cols.astype(jnp.float32) + 0.5) / extent_z - 0.5

    def exchange(values):
        return lax.all_to_all(values, "grid", split_axis=2, concat_axis=2, tiled=True)

    arrived = [
        exchange(contract("dgpcx,tcxyz->tdgpyz", inverse_x[:, :, chunk], start))
        for chunk in range(chunks)
    ]
    final = None
    for chunk in range(chunks):
        low = chunk * depth
        spaced = contract("ekdsy,tdspyz->tepkz", inverse_y, arrived[chunk])
        field = contract("ekdz,tdpyz->tepyk", inverse_z, spaced)
        field_real, field_imag = (field[:, 0], field[:, 1])
        potential = trap_strength * (
            pos_x[low : low + depth, None, None] ** 2
            + pos_y[None, :, None] ** 2
            + pos_z[None, None, :] ** 2
        )
        density = field_real * field_real + field_imag * field_imag
        energy = potential + coupling * density - chem_potential
        decay = jnp.exp(-damping * energy * time_step)
        cosine, sine = cos_sin(jnp.minimum(energy * time_step, 4096.0))
        evo_real = decay * cosine
        evo_imag = -decay * sine
        kick = noise_amp * noise[:, :, low : low + depth]
        moved = jnp.stack(
            [
                field_real * evo_real - field_imag * evo_imag + kick[:, 0],
                field_real * evo_imag + field_imag * evo_real + kick[:, 1],
            ],
            axis=1,
        )
        partial_fwd = contract("ekdz,tdpyz->tepyk", forward_z, moved)
        partial_fwd = contract("egkdy,tdpyz->tegpkz", forward_y, partial_fwd)
        returned = exchange(partial_fwd)
        piece = contract("ekdsp,tdspyz->tekyz", forward_x[:, :, :, :, chunk], returned)
        final = piece if final is None else final + piece
    out = final * kept
    occupation = jnp.sum(out * out, axis=(0, 1))
    local_hist = shell_sums(occupation, modes_x, modes_y, modes_z, 2 * quarter * quarter)
    total_hist = lax.psum(local_hist, ("traj", "grid"))
    traj_count = psi_modes.shape[0] * lax.axis_size("traj")
    momentum_hist = total_hist * (SHELLS / (traj_count * extent_x * extent_y * extent_z))
    filler = jnp.zeros(out.shape[:-1] + (extent_z - 2 * quarter,), jnp.float32)
    psi_next = jnp.concatenate([out[..., :quarter], filler, out[..., quarter:]], axis=-1)
    return (psi_next, momentum_hist)


def solution(mesh):
    placed = (
        P("traj", None, None, "grid", None),
        P("traj", None, "grid", None, None),
        P(None, "grid", None),
    )
    return jax.shard_map(
        shards,
        mesh=mesh,
        in_specs=placed,
        out_specs=(P("traj", None, None, "grid", None), P()),
        check_vma=False,
    )
```

profile of v0, /device:TPU:10, one launch (start us, length us, event | category | flops | bytes accessed | tf_op | source)
XLA Modules:
  0.0 574.9 jit_solution(2185708760382104908)
XLA Ops:
  0.8 4.9 fusion.186
  5.8 9.4 %slice_bitcast_fusion.1 = (f32[2,256,32,64]{3,2,1,0:T(8,128)S(1)}, f32[2,256,32,64]{3,2,1,0:T(8,128)}) fusion(f32[1,2,256,32,256]{4,3,2,1,0:T(8,128)} %param.3), kind=kLoop, calls=%fused_computation.15 | loop fusion | bytes 16777216 | tf_op jit(solution)/shard_map/concatenate | solution.py:110
  17.5 5.5 fusion
  23.1 7.0 %fusion.104 = f32[1,2,8,8,32,128]{5,3,2,1,4,0:T(8,128)S(1)} fusion(f32[2,256,32,128,1,1]{3,2,1,0,5,4:T(8,128)S(1)} %fusion, f32[2,8,4,8,2,256]{5,3,4,1,0,2:T(8,128)S(1)} %maximum_maximum_fusion), kind=kOutput, calls=%fused_computation.202 | convolution fusion | flops 1610612736 | bytes 10747904 | tf_op jit(solution)/shard_map/dgpcx,tcxyz->tdgpyz/dot_general | solution.py:52
  31.7 5.5 all-to-all-start.2
  37.2 9.9 %fusion.101 = f32[1,2,8,8,32,128]{5,3,2,1,4,0:T(8,128)S(1)} fusion(f32[2,256,32,128,1,1]{3,2,1,0,5,4:T(8,128)} %copy-done, f32[2,8,4,8,2,256]{5,3,4,1,0,2:T(8,128)S(1)} %maximum_maximum_fusion), kind=kOutput, calls=%fused_computation.201 | convolution fusion | flops 1610612736 | bytes 10747904 | tf_op jit(solution)/shard_map/dgpcx,tcxyz->tdgpyz/dot_general | solution.py:52
  48.7 34.0 %all-to-all-done.2 = f32[1,2,8,8,32,128]{5,3,1,4,0,2:T(8,128)S(1)} async-done(((f32[1,2,8,8,32,128]{5,3,1,4,0,2:T(8,128)}), f32[1,2,8,8,32,128]{5,3,1,4,0,2:T(8,128)S(1)}, u32[]{:S(2)}, u32[]{:S(2)}) %all-to-all-start.2) | async-done | bytes 2097184 | tf_op jit(solution)/shard_map/all_to_all | solution.py:143
  84.2 8.1 %all-to-all-start = ((f32[1,2,8,8,32,128]{5,3,1,4,0,2:T(8,128)}), f32[1,2,8,8,32,128]{5,3,1,4,0,2:T(8,128)}, u32[]{:S(2)}, u32[]{:S(2)}) async-start(f32[1,2,8,8,32,128]{5,3,1,4,0,2:T(8,128)} %copy.123), calls=%async_computation | async-start | bytes 4194304 | tf_op jit(solution)/shard_map/all_to_all | solution.py:143
  92.2 9.9 %fusion.110 = f32[1,2,8,8,32,128]{5,3,2,1,4,0:T(8,128)S(1)} fusion(f32[2,256,32,128,1,1]{3,2,1,0,5,4:T(8,128)} %copy-done, f32[2,8,4,8,2,256]{5,3,4,1,0,2:T(8,128)S(1)} %maximum_maximum_fusion), kind=kOutput, calls=%fused_computation.204 | convolution fusion | flops 1610612736 | bytes 10747904 | tf_op jit(solution)/shard_map/dgpcx,tcxyz->tdgpyz/dot_general | solution.py:52
  103.9 11.4 %fusion.107 = f32[1,2,8,8,32,128]{5,3,2,1,4,0:T(8,128)} fusion(f32[2,256,32,128,1,1]{3,2,1,0,5,4:T(8,128)} %copy-done, f32[2,8,4,8,2,256]{5,3,4,1,0,2:T(8,128)S(1)} %maximum_maximum_fusion), kind=kOutput, calls=%fused_computation.203 | convolution fusion | flops 1610612736 | bytes 10747904 | tf_op jit(solution)/shard_map/dgpcx,tcxyz->tdgpyz/dot_general | solution.py:52
  115.3 22.1 %all-to-all-done = f32[1,2,8,8,32,128]{5,3,1,4,0,2:T(8,128)} async-done(((f32[1,2,8,8,32,128]{5,3,1,4,0,2:T(8,128)}), f32[1,2,8,8,32,128]{5,3,1,4,0,2:T(8,128)}, u32[]{:S(2)}, u32[]{:S(2)}) %all-to-all-start) | async-done | bytes 2097184 | tf_op jit(solution)/shard_map/all_to_all | solution.py:143
  137.4 7.1 %all-to-all-start.6 = ((f32[1,2,8,8,32,128]{5,3,1,4,0,2:T(8,128)}), f32[1,2,8,8,32,128]{5,3,1,4,0,2:T(8,128)S(1)}, u32[]{:S(2)}, u32[]{:S(2)}) async-start(f32[1,2,8,8,32,128]{5,3,1,4,0,2:T(8,128)} %copy.145), calls=%async_computation.6 | async-start | bytes 4194304 | tf_op jit(solution)/shard_map/all_to_all | solution.py:143
  154.2 10.1 %fusion.184 = (f32[1,2,8,256,256]{4,3,2,1,0:T(8,128)}, f32[1,2,8,256,256]{4,3,2,1,0:T(8,128)}, f32[1,2,8,256,256]{4,3,2,1,0:T(8,128)S(1)}, f32[1,2,8,256,256]{4,3,2,1,0:T(8,128)S(1)}) fusion(f32[1,2,32,256,256]{4,3,2,1,0:T(8,128)} %param.4), kind=kLoop, calls=%fused_computation.386 | loop fusion | bytes 33554432 | tf_op jit(solution)/shard_map/slice | solution.py:166
  164.4 4.0 copy_multiply_fusion.2
  168.4 21.7 %all-to-all-done.6 = f32[1,2,8,8,32,128]{5,3,1,4,0,2:T(8,128)S(1)} async-done(((f32[1,2,8,8,32,128]{5,3,1,4,0,2:T(8,128)}), f32[1,2,8,8,32,128]{5,3,1,4,0,2:T(8,128)S(1)}, u32[]{:S(2)}, u32[]{:S(2)}) %all-to-all-start.6) | async-done | bytes 2097184 | tf_op jit(solution)/shard_map/all_to_all | solution.py:143
  190.1 7.7 %all-to-all-start.4 = ((f32[1,2,8,8,32,128]{5,3,1,4,0,2:T(8,128)}), f32[1,2,8,8,32,128]{5,3,1,4,0,2:T(8,128)}, u32[]{:S(2)}, u32[]{:S(2)}) async-start(f32[1,2,8,8,32,128]{5,3,1,4,0,2:T(8,128)} %copy.138), calls=%async_computation.4 | async-start | bytes 4194304 | tf_op jit(solution)/shard_map/all_to_all | solution.py:143
  197.8 4.1 fusion.84
  201.9 4.1 fusion.90
  206.0 3.6 convolution_bitcast_fusion.2
  209.6 3.6 convolution_bitcast_fusion.3
  213.3 10.2 %slice_add_fusion.7 = (f32[1,1,8,256,256]{4,3,1,2,0:T(8,128)S(1)}, f32[1,1,8,256,256]{4,3,1,2,0:T(8,128)S(1)}, f32[1,1,8,256,256]{4,3,1,2,0:T(8,128)}, f32[1,1,8,256,256]{4,3,1,2,0:T(8,128)}) fusion(f32[1,2,8,256,256]{4,3,1,2,0:T(8,128)S(1)} %copy-done.5, f32[1,2,8,256,256]{4,3,1,2,0:T(8,128)S(1)} %convolution_bitcast_fusion.3, ...), kind=kLoop, calls=%fused_computation.136 | loop fusion | flops 61865984 | bytes 25183232 | tf_op jit(solution)/shard_map/add | solution.py:169
  228.8 14.5 %all-to-all-done.4 = f32[1,2,8,8,32,128]{5,3,1,4,0,2:T(8,128)} async-done(((f32[1,2,8,8,32,128]{5,3,1,4,0,2:T(8,128)}), f32[1,2,8,8,32,128]{5,3,1,4,0,2:T(8,128)}, u32[]{:S(2)}, u32[]{:S(2)}) %all-to-all-start.4) | async-done | bytes 2097184 | tf_op jit(solution)/shard_map/all_to_all | solution.py:143
  243.4 7.8 %all-to-all-start.1 = ((f32[1,2,8,8,32,128]{5,4,1,3,0,2:T(8,128)}), f32[1,2,8,8,32,128]{5,4,1,3,0,2:T(8,128)}, u32[]{:S(2)}, u32[]{:S(2)}) async-start(f32[1,2,8,8,32,128]{5,4,1,3,0,2:T(8,128)} %copy.127), calls=%async_computation.1 | async-start | bytes 4194304 | tf_op jit(solution)/shard_map/all_to_all | solution.py:143
  251.2 8.0 %copy_multiply_fusion = (f32[1,2,8,256,256]{4,3,1,2,0:T(8,128)}, f32[1,2,8,256,256]{4,3,1,2,0:T(8,128)}) fusion(f32[1,2,8,256,256]{4,3,2,1,0:T(8,128)} %get-tuple-element.22, f32[1,2,8,256,256]{4,3,2,1,0:T(8,128)} %get-tuple-element.23), kind=kLoop, calls=%fused_computation.41 | loop fusion | flops 2097152 | bytes 16777216 | tf_op jit(solution)/shard_map/mul | solution.py:166
  264.6 32.2 %all-to-all-done.1 = f32[1,2,8,8,32,128]{5,4,1,3,0,2:T(8,128)} async-done(((f32[1,2,8,8,32,128]{5,4,1,3,0,2:T(8,128)}), f32[1,2,8,8,32,128]{5,4,1,3,0,2:T(8,128)}, u32[]{:S(2)}, u32[]{:S(2)}) %all-to-all-start.1) | async-done | bytes 2097184 | tf_op jit(solution)/shard_map/all_to_all | solution.py:143
  296.8 8.0 %all-to-all-start.3 = ((f32[1,2,8,8,32,128]{5,4,1,3,0,2:T(8,128)}), f32[1,2,8,8,32,128]{5,4,1,3,0,2:T(8,128)}, u32[]{:S(2)}, u32[]{:S(2)}) async-start(f32[1,2,8,8,32,128]{5,4,1,3,0,2:T(8,128)} %copy.135), calls=%async_computation.3 | async-start | bytes 4194304 | tf_op jit(solution)/shard_map/all_to_all | solution.py:143
  308.3 4.1 fusion.78
  312.4 3.6 convolution_bitcast_fusion
  316.1 3.6 convolution_bitcast_fusion.1
  319.7 10.0 %slice_add_fusion.1 = (f32[1,1,8,256,256]{4,3,1,2,0:T(8,128)}, f32[1,1,8,256,256]{4,3,1,2,0:T(8,128)}, f32[1,1,8,256,256]{4,3,1,2,0:T(8,128)S(1)}, f32[1,1,8,256,256]{4,3,1,2,0:T(8,128)S(1)}) fusion(f32[1,2,8,256,256]{4,3,1,2,0:T(8,128)S(1)} %copy-done.2, f32[1,2,8,256,256]{4,3,1,2,0:T(8,128)S(1)} %convolution_bitcast_fusion, ...), kind=kLoop, calls=%fused_computation.130 | loop fusion | flops 61865984 | bytes 25183232 | tf_op jit(solution)/shard_map/add | solution.py:169
  335.0 15.4 %all-to-all-done.3 = f32[1,2,8,8,32,128]{5,4,1,3,0,2:T(8,128)} async-done(((f32[1,2,8,8,32,128]{5,4,1,3,0,2:T(8,128)}), f32[1,2,8,8,32,128]{5,4,1,3,0,2:T(8,128)}, u32[]{:S(2)}, u32[]{:S(2)}) %all-to-all-start.3) | async-done | bytes 2097184 | tf_op jit(solution)/shard_map/all_to_all | solution.py:143
  350.3 7.1 %all-to-all-start.5 = ((f32[1,2,8,8,32,128]{5,4,1,3,0,2:T(8,128)}), f32[1,2,8,8,32,128]{5,4,1,3,0,2:T(8,128)S(1)}, u32[]{:S(2)}, u32[]{:S(2)}) async-start(f32[1,2,8,8,32,128]{5,4,1,3,0,2:T(8,128)} %copy.142), calls=%async_computation.5 | async-start | bytes 4194304 | tf_op jit(solution)/shard_map/all_to_all | solution.py:143
  357.4 3.7 fusion.22
  364.6 38.4 %all-to-all-done.5 = f32[1,2,8,8,32,128]{5,4,1,3,0,2:T(8,128)S(1)} async-done(((f32[1,2,8,8,32,128]{5,4,1,3,0,2:T(8,128)}), f32[1,2,8,8,32,128]{5,4,1,3,0,2:T(8,128)S(1)}, u32[]{:S(2)}, u32[]{:S(2)}) %all-to-all-start.5) | async-done | bytes 2097184 | tf_op jit(solution)/shard_map/all_to_all | solution.py:143
  403.0 8.2 %all-to-all-start.7 = ((f32[1,2,8,8,32,128]{5,4,1,3,0,2:T(8,128)}), f32[1,2,8,8,32,128]{5,4,1,3,0,2:T(8,128)}, u32[]{:S(2)}, u32[]{:S(2)}) async-start(f32[1,2,8,8,32,128]{5,4,1,3,0,2:T(8,128)} %copy.149), calls=%async_computation.7 | async-start | bytes 4194304 | tf_op jit(solution)/shard_map/all_to_all | solution.py:143
  411.3 5.3 copy.151
  418.2 8.8 %fusion.86 = f32[32,128,2,256,1,1]{3,1,5,4,2,0:T(8,128)} fusion(f32[1,2,8,8,32,128]{5,4,1,3,0,2:T(8,128)} %all-to-all-done.1, f32[2,256,2,8,4,8]{1,3,5,2,0,4:T(8,128)S(1)} %maximum_maximum_fusion.1), kind=kOutput, calls=%fused_computation.158 | convolution fusion | flops 1610612736 | bytes 10747904 | tf_op jit(solution)/shard_map/ekdsp,tdspyz->tekyz/dot_general | solution.py:52
  427.0 8.8 %fusion.80 = f32[32,128,2,256,1,1]{3,1,5,4,2,0:T(8,128)} fusion(f32[1,2,8,8,32,128]{5,4,1,3,0,2:T(8,128)} %all-to-all-done.3, f32[2,256,2,8,4,8]{1,3,5,2,0,4:T(8,128)S(1)} %maximum_maximum_fusion.1), kind=kOutput, calls=%fused_computation.152 | convolution fusion | flops 1610612736 | bytes 10747904 | tf_op jit(solution)/shard_map/ekdsp,tdspyz->tekyz/dot_general | solution.py:52
  435.8 6.8 %fusion.74 = f32[32,128,2,256,1,1]{3,1,5,4,2,0:T(8,128)} fusion(f32[1,2,8,8,32,128]{5,4,1,3,0,2:T(8,128)S(1)} %all-to-all-done.5, f32[2,256,2,8,4,8]{1,3,5,2,0,4:T(8,128)S(1)} %maximum_maximum_fusion.1), kind=kOutput, calls=%fused_computation.146 | convolution fusion | flops 1610612736 | bytes 10747904 | tf_op jit(solution)/shard_map/ekdsp,tdspyz->tekyz/dot_general | solution.py:52
  442.6 14.1 %all-to-all-done.7 = f32[1,2,8,8,32,128]{5,4,1,3,0,2:T(8,128)} async-done(((f32[1,2,8,8,32,128]{5,4,1,3,0,2:T(8,128)}), f32[1,2,8,8,32,128]{5,4,1,3,0,2:T(8,128)}, u32[]{:S(2)}, u32[]{:S(2)}) %all-to-all-start.7) | async-done | bytes 2097184 | tf_op jit(solution)/shard_map/all_to_all | solution.py:143
  456.7 18.4 %multiply_reduce_fusion = (f32[256,32,128]{0,2,1:T(8,128)}, f32[1,2,256,32,128]{2,4,1,3,0:T(8,128)}) fusion(f32[256,32,128]{0,2,1:T(8,128)} %copy.151, f32[2,256,2,8,4,8]{1,3,5,2,0,4:T(8,128)S(1)} %maximum_maximum_fusion.1, f32[1,2,8,8,32,128]{5,4,1,3,0,2:T(8,128)} %all-to-all-done.7, f32[32,128,2,256,1,1]{3,1,5,4,2,0:T(8,128)} %fusion.74, ...), kind=kOutput, calls=%fused_computation.13 | convolution fusion | flops 1622147072 | bytes 44302336 | tf_op jit(solution)/shard_map/ekdsp,tdspyz->tekyz/dot_general | solution.py:52
  475.1 5.5 copy.154
  480.5 5.9 %bitcast_select_fusion.1 = (f32[8192,128]{1,0:T(8,128)S(1)}, f32[8192,128]{1,0:T(8,128)S(1)}) fusion(f32[256,32,128]{2,1,0:T(8,128)} %copy.154, s32[128]{0:T(128)S(1)} %and_select_fusion, s32[8192]{0:T(1024)S(1)} %get-tuple-element.47), kind=kLoop, calls=%fused_computation.46 | loop fusion | flops 4194304 | bytes 12616192 | tf_op jit(solution)/shard_map/jit(_where)/select_n | solution.py:85
  491.8 43.2 %psum.7 = f32[128]{0:T(128)S(1)} all-reduce(f32[128]{0:T(128)S(1)} %select_reduce_fusion), channel_id=1, replica_groups=mesh['traj'=4,'grid'=8] {'traj','grid'}, use_global_device_ids=true, to_apply=%region_2.3 | all-reduce | flops 128 | bytes 1024 | tf_op jit(solution)/shard_map/psum | solution.py:182
  535.5 7.8 %fusion.185 = (f32[1,2,256,32,64]{2,4,1,3,0:T(8,128)}, f32[1,2,256,32,64]{2,4,1,3,0:T(8,128)}) fusion(f32[1,2,256,32,128]{2,4,1,3,0:T(8,128)} %get-tuple-element.89), kind=kLoop, calls=%fused_computation.387 | loop fusion | bytes 16777216 | tf_op jit(solution)/shard_map/slice | solution.py:186
  543.3 9.2 %copy.152 = f32[1,2,256,32,64]{4,3,2,1,0:T(8,128)} copy(f32[1,2,256,32,64]{2,4,1,3,0:T(8,128)} %get-tuple-element.36) | data formatting | bytes 8388608 | tf_op jit(solution)/shard_map/slice | solution.py:186
  552.6 9.2 %copy.153 = f32[1,2,256,32,64]{4,3,2,1,0:T(8,128)} copy(f32[1,2,256,32,64]{2,4,1,3,0:T(8,128)} %get-tuple-element.37) | data formatting | bytes 8388608 | tf_op jit(solution)/shard_map/slice | solution.py:186
  561.7 13.0 %pad_maximum_fusion = f32[1,2,256,32,256]{4,3,2,1,0:T(8,128)} fusion(f32[1,2,256,32,64]{4,3,2,1,0:T(8,128)} %copy.153, f32[1,2,256,32,64]{4,3,2,1,0:T(8,128)} %copy.152, f32[256]{0:T(256)S(1)} %pad.5.clone), kind=kLoop, calls=%fused_computation | loop fusion | flops 8388608 | bytes 25166848 | tf_op jit(solution)/shard_map/concatenate | solution.py:186
  (103 shorter events, 49.0 us)
Async XLA Ops:
  16.3 6.8 %copy-start.1 = (f32[256,32,128]{2,1,0:T(8,128)}, f32[256,32,128]{2,1,0:T(8,128)S(1)}, u32[]{:S(2)}) copy-start(f32[256,32,128]{2,1,0:T(8,128)S(1)} %add_convert_fusion) | copy-start | bytes 12582916
  23.1 7.1 %copy-start = (f32[2,256,32,128,1,1]{3,2,1,0,5,4:T(8,128)}, f32[2,256,32,128,1,1]{3,2,1,0,5,4:T(8,128)S(1)}, u32[]{:S(2)}) copy-start(f32[2,256,32,128,1,1]{3,2,1,0,5,4:T(8,128)S(1)} %fusion) | copy-start | bytes 25165828
  31.7 51.1 %all-to-all-start.2 = ((f32[1,2,8,8,32,128]{5,3,1,4,0,2:T(8,128)}), f32[1,2,8,8,32,128]{5,3,1,4,0,2:T(8,128)S(1)}, u32[]{:S(2)}, u32[]{:S(2)}) async-start(f32[1,2,8,8,32,128]{5,3,1,4,0,2:T(8,128)} %copy.131), calls=%async_computation.2 | async-start | bytes 4194304 | tf_op jit(solution)/shard_map/all_to_all | solution.py:143
  82.8 1.4 copy-start.6
  84.2 53.3 %all-to-all-start = ((f32[1,2,8,8,32,128]{5,3,1,4,0,2:T(8,128)}), f32[1,2,8,8,32,128]{5,3,1,4,0,2:T(8,128)}, u32[]{:S(2)}, u32[]{:S(2)}) async-start(f32[1,2,8,8,32,128]{5,3,1,4,0,2:T(8,128)} %copy.123), calls=%async_computation | async-start | bytes 4194304 | tf_op jit(solution)/shard_map/all_to_all | solution.py:143
  137.4 52.7 %all-to-all-start.6 = ((f32[1,2,8,8,32,128]{5,3,1,4,0,2:T(8,128)}), f32[1,2,8,8,32,128]{5,3,1,4,0,2:T(8,128)S(1)}, u32[]{:S(2)}, u32[]{:S(2)}) async-start(f32[1,2,8,8,32,128]{5,3,1,4,0,2:T(8,128)} %copy.145), calls=%async_computation.6 | async-start | bytes 4194304 | tf_op jit(solution)/shard_map/all_to_all | solution.py:143
  190.1 53.3 %all-to-all-start.4 = ((f32[1,2,8,8,32,128]{5,3,1,4,0,2:T(8,128)}), f32[1,2,8,8,32,128]{5,3,1,4,0,2:T(8,128)}, u32[]{:S(2)}, u32[]{:S(2)}) async-start(f32[1,2,8,8,32,128]{5,3,1,4,0,2:T(8,128)} %copy.138), calls=%async_computation.4 | async-start | bytes 4194304 | tf_op jit(solution)/shard_map/all_to_all | solution.py:143
  197.8 4.1 copy-start.9
  201.9 4.1 copy-start.17
  201.9 4.1 copy-start.19
  206.0 7.2 %copy-start.5 = (f32[1,2,8,256,256]{4,3,1,2,0:T(8,128)S(1)}, f32[1,2,8,256,256]{4,3,1,2,0:T(8,128)}, u32[]{:S(2)}) copy-start(f32[1,2,8,256,256]{4,3,1,2,0:T(8,128)} %get-tuple-element.96) | copy-start | bytes 12582916
  209.6 3.6 copy-start.4
  213.2 10.2 %copy-start.11 = (f32[1,128,2,256]{3,1,2,0:T(8,128)S(1)}, f32[1,128,2,256]{3,1,2,0:T(8,128)}, u32[]{:S(2)}) copy-start(f32[1,128,2,256]{3,1,2,0:T(8,128)} %get-tuple-element.42) | copy-start | bytes 786436
  213.3 10.2 %copy-start.14 = (f32[1,128,2,256]{3,1,2,0:T(8,128)S(1)}, f32[1,128,2,256]{3,1,2,0:T(8,128)}, u32[]{:S(2)}) copy-start(f32[1,128,2,256]{3,1,2,0:T(8,128)} %get-tuple-element.43) | copy-start | bytes 786436
  243.4 53.4 %all-to-all-start.1 = ((f32[1,2,8,8,32,128]{5,4,1,3,0,2:T(8,128)}), f32[1,2,8,8,32,128]{5,4,1,3,0,2:T(8,128)}, u32[]{:S(2)}, u32[]{:S(2)}) async-start(f32[1,2,8,8,32,128]{5,4,1,3,0,2:T(8,128)} %copy.127), calls=%async_computation.1 | async-start | bytes 4194304 | tf_op jit(solution)/shard_map/all_to_all | solution.py:143
  251.2 8.1 %copy-start.7 = (f32[1,1,8,256,256]{4,3,1,2,0:T(8,128)S(1)}, f32[1,1,8,256,256]{4,3,1,2,0:T(8,128)}, u32[]{:S(2)}) copy-start(f32[1,1,8,256,256]{4,3,1,2,0:T(8,128)} %get-tuple-element.72) | copy-start | bytes 6291460
  251.2 8.1 %copy-start.8 = (f32[1,1,8,256,256]{4,3,1,2,0:T(8,128)S(1)}, f32[1,1,8,256,256]{4,3,1,2,0:T(8,128)}, u32[]{:S(2)}) copy-start(f32[1,1,8,256,256]{4,3,1,2,0:T(8,128)} %get-tuple-element.73) | copy-start | bytes 6291460
  251.2 8.1 %copy-start.12 = (f32[1,128,2,256]{3,1,2,0:T(8,128)S(1)}, f32[1,128,2,256]{3,1,2,0:T(8,128)}, u32[]{:S(2)}) copy-start(f32[1,128,2,256]{3,1,2,0:T(8,128)} %get-tuple-element.42) | copy-start | bytes 786436
  251.2 8.1 %copy-start.15 = (f32[1,128,2,256]{3,1,2,0:T(8,128)S(1)}, f32[1,128,2,256]{3,1,2,0:T(8,128)}, u32[]{:S(2)}) copy-start(f32[1,128,2,256]{3,1,2,0:T(8,128)} %get-tuple-element.43) | copy-start | bytes 786436
  296.8 53.6 %all-to-all-start.3 = ((f32[1,2,8,8,32,128]{5,4,1,3,0,2:T(8,128)}), f32[1,2,8,8,32,128]{5,4,1,3,0,2:T(8,128)}, u32[]{:S(2)}, u32[]{:S(2)}) async-start(f32[1,2,8,8,32,128]{5,4,1,3,0,2:T(8,128)} %copy.135), calls=%async_computation.3 | async-start | bytes 4194304 | tf_op jit(solution)/shard_map/all_to_all | solution.py:143
  304.8 3.5 copy-start.10
  308.3 4.1 copy-start.18
  308.3 4.1 copy-start.20
  312.4 7.2 %copy-start.3 = (f32[1,2,8,256,256]{4,3,1,2,0:T(8,128)S(1)}, f32[1,2,8,256,256]{4,3,1,2,0:T(8,128)}, u32[]{:S(2)}) copy-start(f32[1,2,8,256,256]{4,3,1,2,0:T(8,128)} %get-tuple-element.94) | copy-start | bytes 12582916
  316.0 3.6 copy-start.2
  319.7 10.0 %copy-start.13 = (f32[1,128,2,256]{3,1,2,0:T(8,128)S(1)}, f32[1,128,2,256]{3,1,2,0:T(8,128)}, u32[]{:S(2)}) copy-start(f32[1,128,2,256]{3,1,2,0:T(8,128)} %get-tuple-element.42) | copy-start | bytes 786436
  319.7 10.0 %copy-start.16 = (f32[1,128,2,256]{3,1,2,0:T(8,128)S(1)}, f32[1,128,2,256]{3,1,2,0:T(8,128)}, u32[]{:S(2)}) copy-start(f32[1,128,2,256]{3,1,2,0:T(8,128)} %get-tuple-element.43) | copy-start | bytes 786436
  350.3 52.7 %all-to-all-start.5 = ((f32[1,2,8,8,32,128]{5,4,1,3,0,2:T(8,128)}), f32[1,2,8,8,32,128]{5,4,1,3,0,2:T(8,128)S(1)}, u32[]{:S(2)}, u32[]{:S(2)}) async-start(f32[1,2,8,8,32,128]{5,4,1,3,0,2:T(8,128)} %copy.142), calls=%async_computation.5 | async-start | bytes 4194304 | tf_op jit(solution)/shard_map/all_to_all | solution.py:143
  403.0 53.7 %all-to-all-start.7 = ((f32[1,2,8,8,32,128]{5,4,1,3,0,2:T(8,128)}), f32[1,2,8,8,32,128]{5,4,1,3,0,2:T(8,128)}, u32[]{:S(2)}, u32[]{:S(2)}) async-start(f32[1,2,8,8,32,128]{5,4,1,3,0,2:T(8,128)} %copy.149), calls=%async_computation.7 | async-start | bytes 4194304 | tf_op jit(solution)/shard_map/all_to_all | solution.py:143
where the time goes:
time: 582 us; the launch traced here: 575 us
  waiting for transfers between devices  192 us (33%)
  matrix products  131 us (23%)
  local copies, waits for them, and re-layouts  77.7 us (13%)
  other arithmetic  69.2 us (12%)
  starting transfers between devices  59.5 us (10%)
  blocking collectives  43.2 us (7%)
    all_to_all x8, waiting for transfers between devices, exchange(): lax.all_to_all(values, 'grid', split_axis=2, concat_axis=2, tiled=True)  192 us
    dot_general x24, matrix products, contract(): return jnp.einsum(pattern, table, values, precision=lax.Precision.HIGH)  128 us
    all_to_all x8, starting transfers between devices, exchange(): lax.all_to_all(values, 'grid', split_axis=2, concat_axis=2, tiled=True)  59.5 us
    psum x1, blocking collectives, shards(): total_hist = lax.psum(local_hist, ('traj', 'grid'))  43.2 us
    add x2, other arithmetic, shards(): field_real * evo_real - field_imag * evo_imag + kick[:, 0]  20.2 us
    slice x2, local copies, waits for them, and re-layouts, shards(): out[..., :quarter]  17.1 us
    transpose x8, local copies, waits for them, and re-layouts, contract(): return jnp.einsum(pattern, table, values, precision=lax.Precision.HIGH)  14.1 us
    concatenate x1, other arithmetic, shards(): jnp.concatenate([out[..., :quarter], filler, out[..., quarter:]], axis=-1)  13 us
  transfers between devices with their start and end apart: 8, of which 8 were waited for; matrix products, arithmetic and copies ran while one was open for 30% of the time, Pallas kernels for 0%

commit v1 on v0

--- a/solution.py
+++ b/solution.py
@@ -179,7 +179,7 @@
     out = final * kept
     occupation = jnp.sum(out * out, axis=(0, 1))
     local_hist = shell_sums(occupation, modes_x, modes_y, modes_z, 2 * quarter * quarter)
-    total_hist = lax.psum(local_hist, ("traj", "grid"))
+    total_hist = jnp.sum(lax.all_gather(local_hist, ("traj", "grid")), axis=0)
     traj_count = psi_modes.shape[0] * lax.axis_size("traj")
     momentum_hist = total_hist * (SHELLS / (traj_count * extent_x * extent_y * extent_z))
     filler = jnp.zeros(out.shape[:-1] + (extent_z - 2 * quarter,), jnp.float32)

time: 582 us -> 583 us (level)
  the two profiles are of different devices: /device:TPU:10 before, /device:TPU:0 now
where the time goes in v1:
time: 583 us; the launch traced here: 576 us
  waiting for transfers between devices  220 us (38%)
  matrix products  132 us (23%)
  local copies, waits for them, and re-layouts  78 us (13%)
  other arithmetic  69 us (12%)
  blocking collectives  39.5 us (7%)
  starting transfers between devices  36.5 us (6%)
    all_to_all x8, waiting for transfers between devices, exchange(): lax.all_to_all(values, 'grid', split_axis=2, concat_axis=2, tiled=True)  220 us
    dot_general x24, matrix products, contract(): return jnp.einsum(pattern, table, values, precision=lax.Precision.HIGH)  128 us
    all_gather x1, blocking collectives, shards(): total_hist = jnp.sum(lax.all_gather(local_hist, ('traj', 'grid')), axis=0)  39.5 us
    all_to_all x8, starting transfers between devices, exchange(): lax.all_to_all(values, 'grid', split_axis=2, concat_axis=2, tiled=True)  36.5 us
    add x2, other arithmetic, shards(): field_real * evo_real - field_imag * evo_imag + kick[:, 0]  20.1 us
    slice x2, local copies, waits for them, and re-layouts, shards(): out[..., :quarter]  17.3 us
    transpose x8, local copies, waits for them, and re-layouts, contract(): return jnp.einsum(pattern, table, values, precision=lax.Precision.HIGH)  14.1 us
    concatenate x1, other arithmetic, shards(): jnp.concatenate([out[..., :quarter], filler, out[..., quarter:]], axis=-1)  13 us
  transfers between devices with their start and end apart: 8, of which 8 were waited for; matrix products, arithmetic and copies ran while one was open for 30% of the time, Pallas kernels for 0%

profile of v1, /device:TPU:0, one launch (start us, length us, event | category | flops | bytes accessed | tf_op | source)
XLA Modules:
  0.0 576.2 jit_solution(5715232873066424755)
XLA Ops:
  0.8 4.9 fusion.186
  5.8 9.4 %slice_bitcast_fusion.1 = (f32[2,256,32,64]{3,2,1,0:T(8,128)S(1)}, f32[2,256,32,64]{3,2,1,0:T(8,128)}) fusion(f32[1,2,256,32,256]{4,3,2,1,0:T(8,128)} %param.3), kind=kLoop, calls=%fused_computation.15 | loop fusion | bytes 16777216 | tf_op jit(solution)/shard_map/concatenate | solution.py:110
  17.5 5.3 fusion
  22.9 7.0 %fusion.104 = f32[1,2,8,8,32,128]{5,3,2,1,4,0:T(8,128)S(1)} fusion(f32[2,256,32,128,1,1]{3,2,1,0,5,4:T(8,128)S(1)} %fusion, f32[2,8,4,8,2,256]{5,3,4,1,0,2:T(8,128)S(1)} %maximum_maximum_fusion), kind=kOutput, calls=%fused_computation.202 | convolution fusion | flops 1610612736 | bytes 10747904 | tf_op jit(solution)/shard_map/dgpcx,tcxyz->tdgpyz/dot_general | solution.py:52
  31.5 7.0 %all-to-all-start.2 = ((f32[1,2,8,8,32,128]{5,3,1,4,0,2:T(8,128)}), f32[1,2,8,8,32,128]{5,3,1,4,0,2:T(8,128)S(1)}, u32[]{:S(2)}, u32[]{:S(2)}) async-start(f32[1,2,8,8,32,128]{5,3,1,4,0,2:T(8,128)} %copy.131), calls=%async_computation.2 | async-start | bytes 4194304 | tf_op jit(solution)/shard_map/all_to_all | solution.py:143
  38.5 9.9 %fusion.101 = f32[1,2,8,8,32,128]{5,3,2,1,4,0:T(8,128)S(1)} fusion(f32[2,256,32,128,1,1]{3,2,1,0,5,4:T(8,128)} %copy-done, f32[2,8,4,8,2,256]{5,3,4,1,0,2:T(8,128)S(1)} %maximum_maximum_fusion), kind=kOutput, calls=%fused_computation.201 | convolution fusion | flops 1610612736 | bytes 10747904 | tf_op jit(solution)/shard_map/dgpcx,tcxyz->tdgpyz/dot_general | solution.py:52
  50.0 37.5 %all-to-all-done.2 = f32[1,2,8,8,32,128]{5,3,1,4,0,2:T(8,128)S(1)} async-done(((f32[1,2,8,8,32,128]{5,3,1,4,0,2:T(8,128)}), f32[1,2,8,8,32,128]{5,3,1,4,0,2:T(8,128)S(1)}, u32[]{:S(2)}, u32[]{:S(2)}) %all-to-all-start.2) | async-done | bytes 2097184 | tf_op jit(solution)/shard_map/all_to_all | solution.py:143
  88.9 4.5 all-to-all-start
  93.4 9.9 %fusion.110 = f32[1,2,8,8,32,128]{5,3,2,1,4,0:T(8,128)S(1)} fusion(f32[2,256,32,128,1,1]{3,2,1,0,5,4:T(8,128)} %copy-done, f32[2,8,4,8,2,256]{5,3,4,1,0,2:T(8,128)S(1)} %maximum_maximum_fusion), kind=kOutput, calls=%fused_computation.204 | convolution fusion | flops 1610612736 | bytes 10747904 | tf_op jit(solution)/shard_map/dgpcx,tcxyz->tdgpyz/dot_general | solution.py:52
  105.1 11.6 %fusion.107 = f32[1,2,8,8,32,128]{5,3,2,1,4,0:T(8,128)} fusion(f32[2,256,32,128,1,1]{3,2,1,0,5,4:T(8,128)} %copy-done, f32[2,8,4,8,2,256]{5,3,4,1,0,2:T(8,128)S(1)} %maximum_maximum_fusion), kind=kOutput, calls=%fused_computation.203 | convolution fusion | flops 1610612736 | bytes 10747904 | tf_op jit(solution)/shard_map/dgpcx,tcxyz->tdgpyz/dot_general | solution.py:52
  116.7 25.6 %all-to-all-done = f32[1,2,8,8,32,128]{5,3,1,4,0,2:T(8,128)} async-done(((f32[1,2,8,8,32,128]{5,3,1,4,0,2:T(8,128)}), f32[1,2,8,8,32,128]{5,3,1,4,0,2:T(8,128)}, u32[]{:S(2)}, u32[]{:S(2)}) %all-to-all-start) | async-done | bytes 2097184 | tf_op jit(solution)/shard_map/all_to_all | solution.py:143
  142.2 3.6 all-to-all-start.6
  155.6 10.1 %fusion.184 = (f32[1,2,8,256,256]{4,3,2,1,0:T(8,128)}, f32[1,2,8,256,256]{4,3,2,1,0:T(8,128)}, f32[1,2,8,256,256]{4,3,2,1,0:T(8,128)S(1)}, f32[1,2,8,256,256]{4,3,2,1,0:T(8,128)S(1)}) fusion(f32[1,2,32,256,256]{4,3,2,1,0:T(8,128)} %param.4), kind=kLoop, calls=%fused_computation.386 | loop fusion | bytes 33554432 | tf_op jit(solution)/shard_map/slice | solution.py:166
  165.7 4.0 copy_multiply_fusion.2
  169.7 25.1 %all-to-all-done.6 = f32[1,2,8,8,32,128]{5,3,1,4,0,2:T(8,128)S(1)} async-done(((f32[1,2,8,8,32,128]{5,3,1,4,0,2:T(8,128)}), f32[1,2,8,8,32,128]{5,3,1,4,0,2:T(8,128)S(1)}, u32[]{:S(2)}, u32[]{:S(2)}) %all-to-all-start.6) | async-done | bytes 2097184 | tf_op jit(solution)/shard_map/all_to_all | solution.py:143
  194.8 4.3 all-to-all-start.4
  199.2 4.1 fusion.84
  203.3 4.1 fusion.90
  207.4 3.6 convolution_bitcast_fusion.2
  211.0 3.6 convolution_bitcast_fusion.3
  214.7 10.0 %slice_add_fusion.7 = (f32[1,1,8,256,256]{4,3,1,2,0:T(8,128)S(1)}, f32[1,1,8,256,256]{4,3,1,2,0:T(8,128)S(1)}, f32[1,1,8,256,256]{4,3,1,2,0:T(8,128)}, f32[1,1,8,256,256]{4,3,1,2,0:T(8,128)}) fusion(f32[1,2,8,256,256]{4,3,1,2,0:T(8,128)S(1)} %copy-done.5, f32[1,2,8,256,256]{4,3,1,2,0:T(8,128)S(1)} %convolution_bitcast_fusion.3, ...), kind=kLoop, calls=%fused_computation.136 | loop fusion | flops 61865984 | bytes 25183232 | tf_op jit(solution)/shard_map/add | solution.py:169
  230.0 18.2 %all-to-all-done.4 = f32[1,2,8,8,32,128]{5,3,1,4,0,2:T(8,128)} async-done(((f32[1,2,8,8,32,128]{5,3,1,4,0,2:T(8,128)}), f32[1,2,8,8,32,128]{5,3,1,4,0,2:T(8,128)}, u32[]{:S(2)}, u32[]{:S(2)}) %all-to-all-start.4) | async-done | bytes 2097184 | tf_op jit(solution)/shard_map/all_to_all | solution.py:143
  248.2 4.3 all-to-all-start.1
  252.6 8.0 %copy_multiply_fusion = (f32[1,2,8,256,256]{4,3,1,2,0:T(8,128)}, f32[1,2,8,256,256]{4,3,1,2,0:T(8,128)}) fusion(f32[1,2,8,256,256]{4,3,2,1,0:T(8,128)} %get-tuple-element.22, f32[1,2,8,256,256]{4,3,2,1,0:T(8,128)} %get-tuple-element.23), kind=kLoop, calls=%fused_computation.41 | loop fusion | flops 2097152 | bytes 16777216 | tf_op jit(solution)/shard_map/mul | solution.py:166
  266.0 35.6 %all-to-all-done.1 = f32[1,2,8,8,32,128]{5,4,1,3,0,2:T(8,128)} async-done(((f32[1,2,8,8,32,128]{5,4,1,3,0,2:T(8,128)}), f32[1,2,8,8,32,128]{5,4,1,3,0,2:T(8,128)}, u32[]{:S(2)}, u32[]{:S(2)}) %all-to-all-start.1) | async-done | bytes 2097184 | tf_op jit(solution)/shard_map/all_to_all | solution.py:143
  301.6 4.6 all-to-all-start.3
  309.7 4.1 fusion.78
  313.8 3.6 convolution_bitcast_fusion
  317.4 3.6 convolution_bitcast_fusion.1
  321.0 10.2 %slice_add_fusion.1 = (f32[1,1,8,256,256]{4,3,1,2,0:T(8,128)}, f32[1,1,8,256,256]{4,3,1,2,0:T(8,128)}, f32[1,1,8,256,256]{4,3,1,2,0:T(8,128)S(1)}, f32[1,1,8,256,256]{4,3,1,2,0:T(8,128)S(1)}) fusion(f32[1,2,8,256,256]{4,3,1,2,0:T(8,128)S(1)} %copy-done.2, f32[1,2,8,256,256]{4,3,1,2,0:T(8,128)S(1)} %convolution_bitcast_fusion, ...), kind=kLoop, calls=%fused_computation.130 | loop fusion | flops 61865984 | bytes 25183232 | tf_op jit(solution)/shard_map/add | solution.py:169
  336.5 18.7 %all-to-all-done.3 = f32[1,2,8,8,32,128]{5,4,1,3,0,2:T(8,128)} async-done(((f32[1,2,8,8,32,128]{5,4,1,3,0,2:T(8,128)}), f32[1,2,8,8,32,128]{5,4,1,3,0,2:T(8,128)}, u32[]{:S(2)}, u32[]{:S(2)}) %all-to-all-start.3) | async-done | bytes 2097184 | tf_op jit(solution)/shard_map/all_to_all | solution.py:143
  355.2 3.6 all-to-all-start.5
  358.8 3.7 fusion.22
  366.0 41.8 %all-to-all-done.5 = f32[1,2,8,8,32,128]{5,4,1,3,0,2:T(8,128)S(1)} async-done(((f32[1,2,8,8,32,128]{5,4,1,3,0,2:T(8,128)}), f32[1,2,8,8,32,128]{5,4,1,3,0,2:T(8,128)S(1)}, u32[]{:S(2)}, u32[]{:S(2)}) %all-to-all-start.5) | async-done | bytes 2097184 | tf_op jit(solution)/shard_map/all_to_all | solution.py:143
  407.8 4.5 all-to-all-start.7
  412.4 5.3 copy.151
  419.3 8.8 %fusion.86 = f32[32,128,2,256,1,1]{3,1,5,4,2,0:T(8,128)} fusion(f32[1,2,8,8,32,128]{5,4,1,3,0,2:T(8,128)} %all-to-all-done.1, f32[2,256,2,8,4,8]{1,3,5,2,0,4:T(8,128)S(1)} %maximum_maximum_fusion.1), kind=kOutput, calls=%fused_computation.158 | convolution fusion | flops 1610612736 | bytes 10747904 | tf_op jit(solution)/shard_map/ekdsp,tdspyz->tekyz/dot_general | solution.py:52
  428.1 8.8 %fusion.80 = f32[32,128,2,256,1,1]{3,1,5,4,2,0:T(8,128)} fusion(f32[1,2,8,8,32,128]{5,4,1,3,0,2:T(8,128)} %all-to-all-done.3, f32[2,256,2,8,4,8]{1,3,5,2,0,4:T(8,128)S(1)} %maximum_maximum_fusion.1), kind=kOutput, calls=%fused_computation.152 | convolution fusion | flops 1610612736 | bytes 10747904 | tf_op jit(solution)/shard_map/ekdsp,tdspyz->tekyz/dot_general | solution.py:52
  436.9 6.8 %fusion.74 = f32[32,128,2,256,1,1]{3,1,5,4,2,0:T(8,128)} fusion(f32[1,2,8,8,32,128]{5,4,1,3,0,2:T(8,128)S(1)} %all-to-all-done.5, f32[2,256,2,8,4,8]{1,3,5,2,0,4:T(8,128)S(1)} %maximum_maximum_fusion.1), kind=kOutput, calls=%fused_computation.146 | convolution fusion | flops 1610612736 | bytes 10747904 | tf_op jit(solution)/shard_map/ekdsp,tdspyz->tekyz/dot_general | solution.py:52
  443.8 17.6 %all-to-all-done.7 = f32[1,2,8,8,32,128]{5,4,1,3,0,2:T(8,128)} async-done(((f32[1,2,8,8,32,128]{5,4,1,3,0,2:T(8,128)}), f32[1,2,8,8,32,128]{5,4,1,3,0,2:T(8,128)}, u32[]{:S(2)}, u32[]{:S(2)}) %all-to-all-start.7) | async-done | bytes 2097184 | tf_op jit(solution)/shard_map/all_to_all | solution.py:143
  461.3 18.4 %multiply_reduce_fusion = (f32[256,32,128]{0,2,1:T(8,128)}, f32[1,2,256,32,128]{2,4,1,3,0:T(8,128)}) fusion(f32[256,32,128]{0,2,1:T(8,128)} %copy.151, f32[2,256,2,8,4,8]{1,3,5,2,0,4:T(8,128)S(1)} %maximum_maximum_fusion.1, f32[1,2,8,8,32,128]{5,4,1,3,0,2:T(8,128)} %all-to-all-done.7, f32[32,128,2,256,1,1]{3,1,5,4,2,0:T(8,128)} %fusion.74, ...), kind=kOutput, calls=%fused_computation.13 | convolution fusion | flops 1622147072 | bytes 44302336 | tf_op jit(solution)/shard_map/ekdsp,tdspyz->tekyz/dot_general | solution.py:52
  479.7 5.5 copy.154
  485.2 5.9 %bitcast_select_fusion.1 = (f32[8192,128]{1,0:T(8,128)S(1)}, f32[8192,128]{1,0:T(8,128)S(1)}) fusion(f32[256,32,128]{2,1,0:T(8,128)} %copy.154, s32[128]{0:T(128)S(1)} %and_select_fusion, s32[8192]{0:T(1024)S(1)} %get-tuple-element.47), kind=kLoop, calls=%fused_computation.46 | loop fusion | flops 4194304 | bytes 12616192 | tf_op jit(solution)/shard_map/jit(_where)/select_n | solution.py:85
  496.4 39.5 %all-gather.1 = f32[32,1,128]{2,1,0:T(1,128)S(1)} all-gather(f32[1,1,128]{2,1,0:T(1,128)S(1)} %bitcast.371), channel_id=2, replica_groups=mesh['traj'=4,'grid'=8] {'traj','grid'}, dimensions={0}, use_global_device_ids=true | all-gather | bytes 16896 | tf_op jit(solution)/shard_map/all_gather | solution.py:182
  536.5 7.8 %fusion.185 = (f32[1,2,256,32,64]{2,4,1,3,0:T(8,128)}, f32[1,2,256,32,64]{2,4,1,3,0:T(8,128)}) fusion(f32[1,2,256,32,128]{2,4,1,3,0:T(8,128)} %get-tuple-element.89), kind=kLoop, calls=%fused_computation.387 | loop fusion | bytes 16777216 | tf_op jit(solution)/shard_map/slice | solution.py:186
  544.3 9.5 %copy.152 = f32[1,2,256,32,64]{4,3,2,1,0:T(8,128)} copy(f32[1,2,256,32,64]{2,4,1,3,0:T(8,128)} %get-tuple-element.36) | data formatting | bytes 8388608 | tf_op jit(solution)/shard_map/slice | solution.py:186
  553.8 9.2 %copy.153 = f32[1,2,256,32,64]{4,3,2,1,0:T(8,128)} copy(f32[1,2,256,32,64]{2,4,1,3,0:T(8,128)} %get-tuple-element.37) | data formatting | bytes 8388608 | tf_op jit(solution)/shard_map/slice | solution.py:186
  563.0 13.0 %pad_maximum_fusion = f32[1,2,256,32,256]{4,3,2,1,0:T(8,128)} fusion(f32[1,2,256,32,64]{4,3,2,1,0:T(8,128)} %copy.153, f32[1,2,256,32,64]{4,3,2,1,0:T(8,128)} %copy.152, f32[256]{0:T(256)S(1)} %pad.5.clone), kind=kLoop, calls=%fused_computation | loop fusion | flops 8388608 | bytes 25166848 | tf_op jit(solution)/shard_map/concatenate | solution.py:186
  (104 shorter events, 49.1 us)
Async XLA Ops:
  16.3 6.6 %copy-start.1 = (f32[256,32,128]{2,1,0:T(8,128)}, f32[256,32,128]{2,1,0:T(8,128)S(1)}, u32[]{:S(2)}) copy-start(f32[256,32,128]{2,1,0:T(8,128)S(1)} %add_convert_fusion) | copy-start | bytes 12582916
  22.9 7.0 %copy-start = (f32[2,256,32,128,1,1]{3,2,1,0,5,4:T(8,128)}, f32[2,256,32,128,1,1]{3,2,1,0,5,4:T(8,128)S(1)}, u32[]{:S(2)}) copy-start(f32[2,256,32,128,1,1]{3,2,1,0,5,4:T(8,128)S(1)} %fusion) | copy-start | bytes 25165828
  31.5 56.0 %all-to-all-start.2 = ((f32[1,2,8,8,32,128]{5,3,1,4,0,2:T(8,128)}), f32[1,2,8,8,32,128]{5,3,1,4,0,2:T(8,128)S(1)}, u32[]{:S(2)}, u32[]{:S(2)}) async-start(f32[1,2,8,8,32,128]{5,3,1,4,0,2:T(8,128)} %copy.131), calls=%async_computation.2 | async-start | bytes 4194304 | tf_op jit(solution)/shard_map/all_to_all | solution.py:143
  87.5 1.4 copy-start.6
  88.9 53.4 %all-to-all-start = ((f32[1,2,8,8,32,128]{5,3,1,4,0,2:T(8,128)}), f32[1,2,8,8,32,128]{5,3,1,4,0,2:T(8,128)}, u32[]{:S(2)}, u32[]{:S(2)}) async-start(f32[1,2,8,8,32,128]{5,3,1,4,0,2:T(8,128)} %copy.123), calls=%async_computation | async-start | bytes 4194304 | tf_op jit(solution)/shard_map/all_to_all | solution.py:143
  142.2 52.6 %all-to-all-start.6 = ((f32[1,2,8,8,32,128]{5,3,1,4,0,2:T(8,128)}), f32[1,2,8,8,32,128]{5,3,1,4,0,2:T(8,128)S(1)}, u32[]{:S(2)}, u32[]{:S(2)}) async-start(f32[1,2,8,8,32,128]{5,3,1,4,0,2:T(8,128)} %copy.145), calls=%async_computation.6 | async-start | bytes 4194304 | tf_op jit(solution)/shard_map/all_to_all | solution.py:143
  194.8 53.4 %all-to-all-start.4 = ((f32[1,2,8,8,32,128]{5,3,1,4,0,2:T(8,128)}), f32[1,2,8,8,32,128]{5,3,1,4,0,2:T(8,128)}, u32[]{:S(2)}, u32[]{:S(2)}) async-start(f32[1,2,8,8,32,128]{5,3,1,4,0,2:T(8,128)} %copy.138), calls=%async_computation.4 | async-start | bytes 4194304 | tf_op jit(solution)/shard_map/all_to_all | solution.py:143
  199.2 4.1 copy-start.9
  203.3 4.1 copy-start.17
  203.3 4.1 copy-start.19
  207.4 7.2 %copy-start.5 = (f32[1,2,8,256,256]{4,3,1,2,0:T(8,128)S(1)}, f32[1,2,8,256,256]{4,3,1,2,0:T(8,128)}, u32[]{:S(2)}) copy-start(f32[1,2,8,256,256]{4,3,1,2,0:T(8,128)} %get-tuple-element.96) | copy-start | bytes 12582916
  211.0 3.6 copy-start.4
  214.6 10.0 %copy-start.11 = (f32[1,128,2,256]{3,1,2,0:T(8,128)S(1)}, f32[1,128,2,256]{3,1,2,0:T(8,128)}, u32[]{:S(2)}) copy-start(f32[1,128,2,256]{3,1,2,0:T(8,128)} %get-tuple-element.42) | copy-start | bytes 786436
  214.6 10.0 %copy-start.14 = (f32[1,128,2,256]{3,1,2,0:T(8,128)S(1)}, f32[1,128,2,256]{3,1,2,0:T(8,128)}, u32[]{:S(2)}) copy-start(f32[1,128,2,256]{3,1,2,0:T(8,128)} %get-tuple-element.43) | copy-start | bytes 786436
  248.2 53.4 %all-to-all-start.1 = ((f32[1,2,8,8,32,128]{5,4,1,3,0,2:T(8,128)}), f32[1,2,8,8,32,128]{5,4,1,3,0,2:T(8,128)}, u32[]{:S(2)}, u32[]{:S(2)}) async-start(f32[1,2,8,8,32,128]{5,4,1,3,0,2:T(8,128)} %copy.127), calls=%async_computation.1 | async-start | bytes 4194304 | tf_op jit(solution)/shard_map/all_to_all | solution.py:143
  252.5 8.1 %copy-start.7 = (f32[1,1,8,256,256]{4,3,1,2,0:T(8,128)S(1)}, f32[1,1,8,256,256]{4,3,1,2,0:T(8,128)}, u32[]{:S(2)}) copy-start(f32[1,1,8,256,256]{4,3,1,2,0:T(8,128)} %get-tuple-element.72) | copy-start | bytes 6291460
  252.6 8.1 %copy-start.8 = (f32[1,1,8,256,256]{4,3,1,2,0:T(8,128)S(1)}, f32[1,1,8,256,256]{4,3,1,2,0:T(8,128)}, u32[]{:S(2)}) copy-start(f32[1,1,8,256,256]{4,3,1,2,0:T(8,128)} %get-tuple-element.73) | copy-start | bytes 6291460
  252.6 8.1 %copy-start.12 = (f32[1,128,2,256]{3,1,2,0:T(8,128)S(1)}, f32[1,128,2,256]{3,1,2,0:T(8,128)}, u32[]{:S(2)}) copy-start(f32[1,128,2,256]{3,1,2,0:T(8,128)} %get-tuple-element.42) | copy-start | bytes 786436
  252.6 8.1 %copy-start.15 = (f32[1,128,2,256]{3,1,2,0:T(8,128)S(1)}, f32[1,128,2,256]{3,1,2,0:T(8,128)}, u32[]{:S(2)}) copy-start(f32[1,128,2,256]{3,1,2,0:T(8,128)} %get-tuple-element.43) | copy-start | bytes 786436
  301.6 53.6 %all-to-all-start.3 = ((f32[1,2,8,8,32,128]{5,4,1,3,0,2:T(8,128)}), f32[1,2,8,8,32,128]{5,4,1,3,0,2:T(8,128)}, u32[]{:S(2)}, u32[]{:S(2)}) async-start(f32[1,2,8,8,32,128]{5,4,1,3,0,2:T(8,128)} %copy.135), calls=%async_computation.3 | async-start | bytes 4194304 | tf_op jit(solution)/shard_map/all_to_all | solution.py:143
  306.2 3.5 copy-start.10
  309.7 4.1 copy-start.18
  309.7 4.1 copy-start.20
  313.8 7.2 %copy-start.3 = (f32[1,2,8,256,256]{4,3,1,2,0:T(8,128)S(1)}, f32[1,2,8,256,256]{4,3,1,2,0:T(8,128)}, u32[]{:S(2)}) copy-start(f32[1,2,8,256,256]{4,3,1,2,0:T(8,128)} %get-tuple-element.94) | copy-start | bytes 12582916
  317.4 3.6 copy-start.2
  321.0 10.2 %copy-start.13 = (f32[1,128,2,256]{3,1,2,0:T(8,128)S(1)}, f32[1,128,2,256]{3,1,2,0:T(8,128)}, u32[]{:S(2)}) copy-start(f32[1,128,2,256]{3,1,2,0:T(8,128)} %get-tuple-element.42) | copy-start | bytes 786436
  321.0 10.2 %copy-start.16 = (f32[1,128,2,256]{3,1,2,0:T(8,128)S(1)}, f32[1,128,2,256]{3,1,2,0:T(8,128)}, u32[]{:S(2)}) copy-start(f32[1,128,2,256]{3,1,2,0:T(8,128)} %get-tuple-element.43) | copy-start | bytes 786436
  355.2 52.6 %all-to-all-start.5 = ((f32[1,2,8,8,32,128]{5,4,1,3,0,2:T(8,128)}), f32[1,2,8,8,32,128]{5,4,1,3,0,2:T(8,128)S(1)}, u32[]{:S(2)}, u32[]{:S(2)}) async-start(f32[1,2,8,8,32,128]{5,4,1,3,0,2:T(8,128)} %copy.142), calls=%async_computation.5 | async-start | bytes 4194304 | tf_op jit(solution)/shard_map/all_to_all | solution.py:143
  407.8 53.6 %all-to-all-start.7 = ((f32[1,2,8,8,32,128]{5,4,1,3,0,2:T(8,128)}), f32[1,2,8,8,32,128]{5,4,1,3,0,2:T(8,128)}, u32[]{:S(2)}, u32[]{:S(2)}) async-start(f32[1,2,8,8,32,128]{5,4,1,3,0,2:T(8,128)} %copy.149), calls=%async_computation.7 | async-start | bytes 4194304 | tf_op jit(solution)/shard_map/all_to_all | solution.py:143
